TPU v7x, 32 devices: a whole 2x2x4 slice. The times are simulated.
32 devices in a mesh: grp: 8 (over y, x, core), shard: 4 (over z).
Axes of the slice: x: 2, y: 2, z: 4, core: 2. Of those that a mesh axis runs over, the one named last changes fastest.
Arguments:
- gradients: bfloat16 [8, 1024, 5120], P('grp', None, 'shard'), may hold values from -150 to 150
- left_factor: bfloat16 [8, 1024, 1024], P('grp'), may hold values from -1 to 2, as said below
- right_factor: bfloat16 [8, 5120, 5120], P('grp', 'shard'), may hold values from -1 to 2, as said below
Outputs:
- update: bfloat16 [8, 1024, 5120], P('grp', None, 'shard')
Inputs may be any that keep to these rules, and one draw needn't show every extreme that they name: `left_factor`: each factor is upper triangular with a positive diagonal. `right_factor`: each factor is upper triangular with a positive diagonal.
All inputs are finite; a program needn't handle non-finite values.
Results may differ from a plain program's by a relative error of at most 0.0061.
Values may be sent and summed in bfloat16 or wider, within the bound.
A program may use at most 128 MiB of HBM per device.

v0:
```python
import jax
import jax.numpy as jnp
from jax import lax
from jax.sharding import PartitionSpec as P


def body(gradients, left_factor, right_factor):
    squares = jnp.float32(0.0)
    gradient = gradients[0]
    left_q = left_factor[0]
    right_rows = right_factor[0]
    block = right_rows
    first = lax.dot_general(
        lax.all_gather(gradient, "shard", axis=1, tiled=True),
        block,
        (((1,), (1,)), ((), ())),
        preferred_element_type=jnp.float32,
    ).astype(jnp.bfloat16)
    block = right_rows
    second_rows = lax.psum_scatter(
        lax.dot_general(block, first, (((0,), (1,)), ((), ())), preferred_element_type=jnp.float32),
        "shard",
        scatter_dimension=0,
        tiled=True,
    ).astype(jnp.bfloat16)
    second = second_rows.T
    third = jnp.dot(left_q, second, preferred_element_type=jnp.float32).astype(jnp.bfloat16)
    precond = lax.dot_general(
        left_q, third, (((0,), (0,)), ((), ())), preferred_element_type=jnp.float32
    )
    results = [precond]
    squares = jnp.sum(precond * precond)
    total = lax.psum(squares, ("grp", "shard"))
    count = (
        gradients.shape[0]
        * lax.axis_size("grp")
        * gradients.shape[1]
        * gradients.shape[2]
        * lax.axis_size("shard")
    )
    rms = jnp.sqrt(total / count + 1e-06)
    factor = jnp.minimum(jnp.float32(1.0), 1.1 / rms)
    stacked = jnp.stack(results, axis=0)
    return (stacked * factor).astype(jnp.bfloat16)


def solution(mesh):
    in_specs = (P("grp", None, "shard"), P("grp", None, None), P("grp", "shard", None))
    out_specs = P("grp", None, "shard")
    return jax.shard_map(body, mesh=mesh, in_specs=in_specs, out_specs=out_specs, check_vma=False)
```

profile of v0, /device:TPU:0, one launch (start us, length us, event | category | flops | bytes accessed | tf_op | source)
XLA Modules:
  0.0 647.6 jit_solution(3090217392802980609)
XLA Ops:
  6.5 0.0 copy-start
  6.5 0.0 all-gather.3.cloned.1.call-start
  6.5 0.7 all-gather.3.cloned.1.call-update
  7.3 0.0 reduce-scatter.2.cloned.1.call-start
  7.3 188.3 %all-gather.3.cloned.1.call-done = bf16[1,1024,5120]{2,1,0:T(8,128)(2,1)} async-done(((bf16[1,1024,1280]{2,1,0:T(8,128)(2,1)}), bf16[1,1024,5120]{2,1,0:T(8,128)(2,1)}) %all-gather.3.cloned.1.call-update) | async-done | bytes 10485776 | tf_op jit(solution)/shard_map/all_gather | solution.py:14
  195.6 17.5 %fusion.8 = bf16[1024,1280]{1,0:T(8,128)(2,1)S(1)} fusion(bf16[1,1280,5120]{2,1,0:T(8,128)(2,1)} %param.5, bf16[1,1024,5120]{2,1,0:T(8,128)(2,1)} %all-gather.3.cloned.1.call-done), kind=kOutput, calls=%fused_computation.8 | convolution fusion | flops 13423083520 | bytes 26214400 | tf_op jit(solution)/shard_map/dot_general | solution.py:13
  213.0 20.6 %fusion.4 = f32[5120,1024]{0,1:T(8,128)} fusion(bf16[1024,1280]{1,0:T(8,128)(2,1)S(1)} %fusion.8, bf16[1,1280,5120]{2,1,0:T(8,128)(2,1)} %param.5), kind=kOutput, calls=%fused_computation.4 | convolution fusion | flops 13421772800 | bytes 36700160 | tf_op jit(solution)/shard_map/dot_general | solution.py:21
  233.6 0.0 reduce-scatter.2.cloned.1.call-update
  233.7 345.7 %reduce-scatter.2.cloned.1.call-done = f32[1280,1024]{0,1:T(8,128)} async-done(((f32[5120,1024]{0,1:T(8,128)}), f32[1280,1024]{0,1:T(8,128)}) %reduce-scatter.2.cloned.1.call-update) | async-done | bytes 5242896 | tf_op jit(solution)/shard_map/reduce_scatter | solution.py:20
  579.4 0.0 copy-done
  579.4 9.9 %multiply_reduce_fusion = (f32[]{:T(128)}, f32[1280,1024]{1,0:T(8,128)}) fusion(bf16[1,1024,1024]{2,1,0:T(8,128)(2,1)S(1)} %copy-done, f32[1280,1024]{0,1:T(8,128)} %reduce-scatter.2.cloned.1.call-done), kind=kOutput, calls=%fused_computation.7 | convolution fusion | flops 5373952000 | bytes 12582916 | tf_op jit(solution)/shard_map/dot_general | solution.py:28
  589.3 41.7 %psum.7 = f32[]{:T(128)} all-reduce(f32[]{:T(128)} %get-tuple-element.5), channel_id=1, replica_groups=mesh['grp'=8,'shard'=4] {'grp','shard'}, use_global_device_ids=true, to_apply=%region_2.0 | all-reduce | flops 1 | bytes 8 | tf_op jit(solution)/shard_map/psum | solution.py:33
  631.7 4.7 fusion.13
  636.4 4.4 copy.4
Async XLA Ops:
  6.5 572.8 %copy-start = (bf16[1,1024,1024]{2,1,0:T(8,128)(2,1)S(1)}, bf16[1,1024,1024]{2,1,0:T(8,128)(2,1)}, u32[]{:S(2)}) copy-start(bf16[1,1024,1024]{2,1,0:T(8,128)(2,1)} %param.4) | copy-start | bytes 6291460
  6.5 189.0 %all-gather.3.cloned.1.call-start = ((), (), s32[]{:S(2)}) async-start(), calls=%async_computation.2 | async-start | bytes 13107200 | tf_op jit(solution)/shard_map/all_gather | solution.py:14
  7.3 572.1 %reduce-scatter.2.cloned.1.call-start = ((), (), s32[]{:S(2)}) async-start(), calls=%async_computation.1 | async-start | bytes 26214400 | tf_op jit(solution)/shard_map/reduce_scatter | solution.py:20
Sparse Core Ops, SparseCore 0:
  8.9 186.6 all-gather.2
  233.8 345.5 reduce-scatter.1
where the time goes:
time: 648 us
  waiting for transfers between devices  535 us (83%)
  matrix products  48 us (7%)
  blocking collectives  41.7 us (6%)
  between operations  14.1 us (2%)
    reduce_scatter x1, waiting for transfers between devices, body(): lax.psum_scatter(lax.dot_general(block, first, (((0,), (1,)), ((), ())),...  346 us
    all_gather x1, waiting for transfers between devices, body(): lax.all_gather(gradient, 'shard', axis=1, tiled=True)  188 us
    psum x1, blocking collectives, body(): total = lax.psum(squares, ('grp', 'shard'))  41.7 us
    dot_general x1, matrix products, body(): lax.dot_general(block, first, (((0,), (1,)), ((), ())), preferred_element...  20.6 us
    dot_general x1, matrix products, body(): lax.dot_general(lax.all_gather(gradient, 'shard', axis=1, tiled=True), bl...  17.5 us
  transfers between devices with their start and end apart: 2, of which 2 were waited for; matrix products, arithmetic and copies ran while one was open for 0% of the time, Pallas kernels for 0%

commit v1 on v0

--- a/solution.py
+++ b/solution.py
@@ -30,7 +30,8 @@
     )
     results = [precond]
     squares = jnp.sum(precond * precond)
-    total = lax.psum(squares, ("grp", "shard"))
+    half = lax.psum(squares, "shard")
+    total = lax.psum(half, "grp")
     count = (
         gradients.shape[0]
         * lax.axis_size("grp")

time: 648 us -> 631 us (0.974)
  blocking collectives: 41.7 us -> 24.8 us
    psum x1 -> x2, blocking collectives: 41.7 us -> 24.8 us  [the longest x1 12.4 us: body(): total = lax.psum(half, 'grp')]
where the time goes in v1:
time: 631 us
  waiting for transfers between devices  535 us (85%)
  matrix products  48 us (8%)
  blocking collectives  24.8 us (4%)
  between operations  14.1 us (2%)
    reduce_scatter x1, waiting for transfers between devices, body(): lax.psum_scatter(lax.dot_general(block, first, (((0,), (1,)), ((), ())),...  346 us
    all_gather x1, waiting for transfers between devices, body(): lax.all_gather(gradient, 'shard', axis=1, tiled=True)  188 us
    dot_general x1, matrix products, body(): lax.dot_general(block, first, (((0,), (1,)), ((), ())), preferred_element...  20.6 us
    dot_general x1, matrix products, body(): lax.dot_general(lax.all_gather(gradient, 'shard', axis=1, tiled=True), bl...  17.5 us
  transfers between devices with their start and end apart: 2, of which 2 were waited for; matrix products, arithmetic and copies ran while one was open for 0% of the time, Pallas kernels for 0%

profile of v1, /device:TPU:0, one launch (start us, length us, event | category | flops | bytes accessed | tf_op | source)
XLA Modules:
  0.0 630.7 jit_solution(1604368660793829187)
XLA Ops:
  6.5 0.0 copy-start
  6.5 0.0 all-gather.3.cloned.1.call-start
  6.5 0.7 all-gather.3.cloned.1.call-update
  7.3 0.0 reduce-scatter.2.cloned.1.call-start
  7.3 188.3 %all-gather.3.cloned.1.call-done = bf16[1,1024,5120]{2,1,0:T(8,128)(2,1)} async-done(((bf16[1,1024,1280]{2,1,0:T(8,128)(2,1)}), bf16[1,1024,5120]{2,1,0:T(8,128)(2,1)}) %all-gather.3.cloned.1.call-update) | async-done | bytes 10485776 | tf_op jit(solution)/shard_map/all_gather | solution.py:14
  195.6 17.5 %fusion.8 = bf16[1024,1280]{1,0:T(8,128)(2,1)S(1)} fusion(bf16[1,1280,5120]{2,1,0:T(8,128)(2,1)} %param.5, bf16[1,1024,5120]{2,1,0:T(8,128)(2,1)} %all-gather.3.cloned.1.call-done), kind=kOutput, calls=%fused_computation.8 | convolution fusion | flops 13423083520 | bytes 26214400 | tf_op jit(solution)/shard_map/dot_general | solution.py:13
  213.0 20.6 %fusion.4 = f32[5120,1024]{0,1:T(8,128)} fusion(bf16[1024,1280]{1,0:T(8,128)(2,1)S(1)} %fusion.8, bf16[1,1280,5120]{2,1,0:T(8,128)(2,1)} %param.5), kind=kOutput, calls=%fused_computation.4 | convolution fusion | flops 13421772800 | bytes 36700160 | tf_op jit(solution)/shard_map/dot_general | solution.py:21
  233.6 0.0 reduce-scatter.2.cloned.1.call-update
  233.7 345.7 %reduce-scatter.2.cloned.1.call-done = f32[1280,1024]{0,1:T(8,128)} async-done(((f32[5120,1024]{0,1:T(8,128)}), f32[1280,1024]{0,1:T(8,128)}) %reduce-scatter.2.cloned.1.call-update) | async-done | bytes 5242896 | tf_op jit(solution)/shard_map/reduce_scatter | solution.py:20
  579.4 0.0 copy-done
  579.4 9.9 %multiply_reduce_fusion = (f32[]{:T(128)}, f32[1280,1024]{1,0:T(8,128)}) fusion(bf16[1,1024,1024]{2,1,0:T(8,128)(2,1)S(1)} %copy-done, f32[1280,1024]{0,1:T(8,128)} %reduce-scatter.2.cloned.1.call-done), kind=kOutput, calls=%fused_computation.7 | convolution fusion | flops 5373952000 | bytes 12582916 | tf_op jit(solution)/shard_map/dot_general | solution.py:28
  589.3 12.4 %psum.14 = f32[]{:T(128)} all-reduce(f32[]{:T(128)} %get-tuple-element.5), channel_id=1, replica_groups=mesh['grp'=8,'shard'=4] {'shard'}, use_global_device_ids=true, to_apply=%region_2.0 | all-reduce | flops 1 | bytes 8 | tf_op jit(solution)/shard_map/psum | solution.py:33
  601.7 12.4 %psum.15 = f32[]{:T(128)} all-reduce(f32[]{:T(128)} %psum.14), channel_id=1, replica_groups=mesh['grp'=8,'shard'=4] {'grp'}, use_global_device_ids=true, to_apply=%region_3.0 | all-reduce | flops 1 | bytes 8 | tf_op jit(solution)/shard_map/psum | solution.py:34
  614.8 4.7 fusion.13
  619.5 4.4 copy.4
Async XLA Ops:
  6.5 572.8 %copy-start = (bf16[1,1024,1024]{2,1,0:T(8,128)(2,1)S(1)}, bf16[1,1024,1024]{2,1,0:T(8,128)(2,1)}, u32[]{:S(2)}) copy-start(bf16[1,1024,1024]{2,1,0:T(8,128)(2,1)} %param.4) | copy-start | bytes 6291460
  6.5 189.0 %all-gather.3.cloned.1.call-start = ((), (), s32[]{:S(2)}) async-start(), calls=%async_computation.2 | async-start | bytes 13107200 | tf_op jit(solution)/shard_map/all_gather | solution.py:14
  7.3 572.1 %reduce-scatter.2.cloned.1.call-start = ((), (), s32[]{:S(2)}) async-start(), calls=%async_computation.1 | async-start | bytes 26214400 | tf_op jit(solution)/shard_map/reduce_scatter | solution.py:20
Sparse Core Ops, SparseCore 0:
  8.9 186.6 all-gather.2
  233.8 345.5 reduce-scatter.1

commit v2 on v0

--- a/solution.py
+++ b/solution.py
@@ -2,6 +2,12 @@
 import jax.numpy as jnp
 from jax import lax
 from jax.sharding import PartitionSpec as P
+
+
+def stack_and_merge(x, mesh_axis, dim):
+    parts = lax.all_gather(x, mesh_axis, axis=0, tiled=False)
+    whole = jnp.concatenate(parts, axis=dim)
+    return whole
 
 
 def body(gradients, left_factor, right_factor):
@@ -11,7 +17,7 @@
     right_rows = right_factor[0]
     block = right_rows
     first = lax.dot_general(
-        lax.all_gather(gradient, "shard", axis=1, tiled=True),
+        stack_and_merge(gradient, "shard", 1),
         block,
         (((1,), (1,)), ((), ())),
         preferred_element_type=jnp.float32,

time: 648 us -> 663 us (1.023)
  local copies, waits for them, and re-layouts: 4.38 us -> 18.8 us
    all_gather x0 -> x1, local copies, waits for them, and re-layouts: none -> 14.4 us  [stack_and_merge(): parts = lax.all_gather(x, mesh_axis, axis=0, tiled=False)]
where the time goes in v2:
time: 663 us; the launch traced here: 662 us
  waiting for transfers between devices  535 us (81%)
  matrix products  48.1 us (7%)
  blocking collectives  41.7 us (6%)
  local copies, waits for them, and re-layouts  18.8 us (3%)
  between operations  14.1 us (2%)
    reduce_scatter x1, waiting for transfers between devices, body(): lax.psum_scatter(lax.dot_general(block, first, (((0,), (1,)), ((), ())),...  346 us
    all_gather x1, waiting for transfers between devices, stack_and_merge(): parts = lax.all_gather(x, mesh_axis, axis=0, tiled=False)  188 us
    psum x1, blocking collectives, body(): total = lax.psum(squares, ('grp', 'shard'))  41.7 us
    dot_general x1, matrix products, body(): lax.dot_general(block, first, (((0,), (1,)), ((), ())), preferred_element...  20.6 us
    dot_general x1, matrix products, body(): lax.dot_general(stack_and_merge(gradient, 'shard', 1), block, (((1,), (1,...  17.6 us
    all_gather x1, local copies, waits for them, and re-layouts, stack_and_merge(): parts = lax.all_gather(x, mesh_axis, axis=0, tiled=False)  14.4 us
  transfers between devices with their start and end apart: 2, of which 2 were waited for; matrix products, arithmetic and copies ran while one was open for 0% of the time, Pallas kernels for 0%

profile of v2, /device:TPU:0, one launch (start us, length us, event | category | flops | bytes accessed | tf_op | source)
XLA Modules:
  0.0 662.1 jit_solution(1887197203822806031)
XLA Ops:
  6.5 0.0 copy-start
  6.5 0.0 all-gather.2.cloned.1.call-start
  6.5 0.7 all-gather.2.cloned.1.call-update
  7.3 0.0 reduce-scatter.2.cloned.1.call-start
  7.3 188.3 %all-gather.2.cloned.1.call-done = bf16[4,1024,1280]{2,1,0:T(8,128)(2,1)} async-done(((bf16[1,1024,1280]{2,1,0:T(8,128)(2,1)}), bf16[4,1024,1280]{2,1,0:T(8,128)(2,1)}) %all-gather.2.cloned.1.call-update) | async-done | bytes 10485776 | tf_op jit(solution)/shard_map/all_gather | solution.py:8
  195.6 14.4 %copy.7 = bf16[4,1024,1280]{1,2,0:T(8,128)(2,1)} copy(bf16[4,1024,1280]{2,1,0:T(8,128)(2,1)} %all-gather.2.cloned.1.call-done) | data formatting | bytes 20971520 | tf_op jit(solution)/shard_map/all_gather | solution.py:8
  209.9 17.6 %fusion.7 = bf16[1024,1280]{1,0:T(8,128)(2,1)S(1)} fusion(bf16[1024,5120]{0,1:T(8,128)(2,1)} %bitcast.31, bf16[1,1280,5120]{2,1,0:T(8,128)(2,1)} %param.5), kind=kOutput, calls=%fused_computation.7 | convolution fusion | flops 13423083520 | bytes 26214400 | tf_op jit(solution)/shard_map/dot_general | solution.py:19
  227.5 20.6 %fusion.4 = f32[5120,1024]{0,1:T(8,128)} fusion(bf16[1024,1280]{1,0:T(8,128)(2,1)S(1)} %fusion.7, bf16[1,1280,5120]{2,1,0:T(8,128)(2,1)} %param.5), kind=kOutput, calls=%fused_computation.4 | convolution fusion | flops 13421772800 | bytes 36700160 | tf_op jit(solution)/shard_map/dot_general | solution.py:27
  248.1 0.0 reduce-scatter.2.cloned.1.call-update
  248.1 345.7 %reduce-scatter.2.cloned.1.call-done = f32[1280,1024]{0,1:T(8,128)} async-done(((f32[5120,1024]{0,1:T(8,128)}), f32[1280,1024]{0,1:T(8,128)}) %reduce-scatter.2.cloned.1.call-update) | async-done | bytes 5242896 | tf_op jit(solution)/shard_map/reduce_scatter | solution.py:26
  593.8 0.0 copy-done
  593.8 9.9 %multiply_reduce_fusion = (f32[]{:T(128)}, f32[1280,1024]{1,0:T(8,128)}) fusion(bf16[1,1024,1024]{2,1,0:T(8,128)(2,1)S(1)} %copy-done, f32[1280,1024]{0,1:T(8,128)} %reduce-scatter.2.cloned.1.call-done), kind=kOutput, calls=%fused_computation.6 | convolution fusion | flops 5373952000 | bytes 12582916 | tf_op jit(solution)/shard_map/dot_general | solution.py:34
  603.8 41.7 %psum.7 = f32[]{:T(128)} all-reduce(f32[]{:T(128)} %get-tuple-element.5), channel_id=1, replica_groups=mesh['grp'=8,'shard'=4] {'grp','shard'}, use_global_device_ids=true, to_apply=%region_2.0 | all-reduce | flops 1 | bytes 8 | tf_op jit(solution)/shard_map/psum | solution.py:39
  646.1 4.7 fusion.10
  650.9 4.4 copy.8
Async XLA Ops:
  6.5 587.3 %copy-start = (bf16[1,1024,1024]{2,1,0:T(8,128)(2,1)S(1)}, bf16[1,1024,1024]{2,1,0:T(8,128)(2,1)}, u32[]{:S(2)}) copy-start(bf16[1,1024,1024]{2,1,0:T(8,128)(2,1)} %param.4) | copy-start | bytes 6291460
  6.5 189.0 %all-gather.2.cloned.1.call-start = ((), (), s32[]{:S(2)}) async-start(), calls=%async_computation.1 | async-start | bytes 13107200 | tf_op jit(solution)/shard_map/all_gather | solution.py:8
  7.3 586.6 %reduce-scatter.2.cloned.1.call-start = ((), (), s32[]{:S(2)}) async-start(), calls=%async_computation.2 | async-start | bytes 26214400 | tf_op jit(solution)/shard_map/reduce_scatter | solution.py:26
Sparse Core Ops, SparseCore 0:
  8.9 186.6 all-gather.1
  248.3 345.5 reduce-scatter.1
